TPU v7x, 128 devices: a whole 4x4x4 slice. The times are simulated.
128 devices in a mesh: dp: 1, sp: 64 (over z, y, x), tp: 2 (over core).
Axes of the slice: x: 4, y: 4, z: 4, core: 2. Of those that a mesh axis runs over, the one named last changes fastest.
Arguments:
- x: bfloat16 [8192, 2048], P(('dp', 'sp', 'tp'))
- segment_ids: int32 [8192], P(('dp', 'sp', 'tp'))
- positions: int32 [8192], P(('dp', 'sp', 'tp'))
- g_attn: bfloat16 [6, 2048], replicated
- w_q: bfloat16 [6, 2048, 16, 128], P(None, None, 'tp')
- w_k: bfloat16 [6, 2048, 2, 128], replicated
- w_v: bfloat16 [6, 2048, 2, 128], replicated
- w_o: bfloat16 [6, 16, 128, 2048], P(None, 'tp')
- g_mlp: bfloat16 [6, 2048], replicated
- w_gate: bfloat16 [6, 2048, 11008], P(None, None, 'tp')
- w_up: bfloat16 [6, 2048, 11008], P(None, None, 'tp')
- w_down: bfloat16 [6, 11008, 2048], P(None, 'tp')
Outputs:
- output: bfloat16 [8192, 2048], P(('dp', 'sp', 'tp'))
All inputs are finite; a program needn't handle non-finite values.
Results may differ from a plain program's by a relative error of at most 0.02.
Values are sent between devices in bfloat16 or wider.
A program may use at most 1.5 GiB of HBM per device.

v0:
```python
import jax
import jax.numpy as jnp
from jax import lax
from jax.sharding import PartitionSpec as P

EPS = 1e-6
ROPE_BASE = 10000.0
WINDOW = 1024
SCORE_ROWS = 256


def rms_norm(x, gain):
    x_wide = x.astype(jnp.float32)
    inv_rms = lax.rsqrt(jnp.mean(x_wide * x_wide, axis=-1, keepdims=True) + EPS)
    return (x_wide * inv_rms * gain.astype(jnp.float32)).astype(jnp.bfloat16)


def rope_tables(positions, head_dim):
    half_width = head_dim // 2
    inv_freq = ROPE_BASE ** (-jnp.arange(half_width, dtype=jnp.float32) / half_width)
    angles = positions.astype(jnp.float32)[:, None] * inv_freq[None, :]
    return jnp.cos(angles)[:, None, :], jnp.sin(angles)[:, None, :]


def rope(t, cos_tab, sin_tab):
    half_width = t.shape[-1] // 2
    t_wide = t.astype(jnp.float32)
    lower_half = t_wide[..., :half_width]
    upper_half = t_wide[..., half_width:]
    return jnp.concatenate([lower_half * cos_tab - upper_half * sin_tab, upper_half * cos_tab + lower_half * sin_tab], axis=-1).astype(jnp.bfloat16)


def attend(q, k_all, v_all, seg_q, seg_all, q_offset, windowed):
    q_rows, kv_count, group_size, head_dim = q.shape
    total = k_all.shape[0]
    block_rows = min(q_rows, max(SCORE_ROWS // (kv_count * group_size), 8))
    blocks = q_rows // block_rows
    key_span = min(block_rows + WINDOW, total) if windowed else total
    q_blocks = q.reshape(blocks, block_rows, kv_count, group_size, head_dim)
    seg_blocks = seg_q.reshape(blocks, block_rows)

    def one_block(block_args):
        q_blk, seg_blk, block_idx = block_args
        q_start = q_offset + block_idx * block_rows
        k_start = jnp.clip(q_start + block_rows - key_span, 0, total - key_span)
        k_blk = lax.dynamic_slice_in_dim(k_all, k_start, key_span, 0)
        v_blk = lax.dynamic_slice_in_dim(v_all, k_start, key_span, 0)
        seg_k = lax.dynamic_slice_in_dim(seg_all, k_start, key_span, 0)
        q_pos = q_start + jnp.arange(block_rows)
        k_pos = k_start + jnp.arange(key_span)
        allowed = (k_pos[None, :] <= q_pos[:, None]) & (seg_k[None, :] == seg_blk[:, None])
        if windowed:
            allowed = allowed & (q_pos[:, None] - k_pos[None, :] < WINDOW)
        scores = jnp.einsum("qgrd,kgd->qgrk", q_blk, k_blk, preferred_element_type=jnp.float32) * head_dim ** -0.5
        scores = jnp.where(allowed[:, None, None, :], scores, -1e30)
        attn_probs = jax.nn.softmax(scores, axis=-1).astype(jnp.bfloat16)
        return jnp.einsum("qgrk,kgd->qgrd", attn_probs, v_blk, preferred_element_type=jnp.float32).astype(jnp.bfloat16)

    out_blocks = lax.map(one_block, (q_blocks, seg_blocks, jnp.arange(blocks)))
    return out_blocks.reshape(q_rows, kv_count * group_size * head_dim)


def matmul(rows_in, weight):
    return jnp.dot(rows_in, weight, preferred_element_type=jnp.float32)


def solution(mesh):
    tp_size = mesh.shape["tp"]
    row_spec = P(("dp", "sp", "tp"), None)
    id_spec = P(("dp", "sp", "tp"))
    whole = P()
    in_specs = (row_spec, id_spec, id_spec, whole, P(None, None, "tp", None), whole, whole, P(None, "tp", None, None), whole, P(None, None, "tp"), P(None, None, "tp"), P(None, "tp", None))

    def local_fn(x, segment_ids, positions, g_attn, w_q, w_k, w_v, w_o, g_mlp, w_gate, w_up, w_down):
        sp_idx = lax.axis_index("sp")
        tp_idx = lax.axis_index("tp")
        layers, model, heads_loc, head_dim = w_q.shape
        kv_heads = w_k.shape[2]
        kv_loc = max(kv_heads // tp_size, 1)
        group_size = heads_loc // kv_loc
        kv_start = tp_idx * kv_heads // tp_size
        seg_all = lax.all_gather(segment_ids, ("sp", "tp"), tiled=True)
        pos_shard = lax.all_gather(positions, "tp", tiled=True)
        shard_rows = pos_shard.shape[0]
        q_offset = sp_idx * shard_rows
        seg_q = lax.dynamic_slice_in_dim(seg_all, q_offset, shard_rows, 0)
        cos_tab, sin_tab = rope_tables(pos_shard, head_dim)
        for layer in range(layers):
            normed = lax.all_gather(rms_norm(x, g_attn[layer]), "tp", tiled=True)
            w_k_loc = lax.dynamic_slice_in_dim(w_k[layer], kv_start, kv_loc, 1).reshape(model, kv_loc * head_dim)
            w_v_loc = lax.dynamic_slice_in_dim(w_v[layer], kv_start, kv_loc, 1).reshape(model, kv_loc * head_dim)
            q = matmul(normed, w_q[layer].reshape(model, heads_loc * head_dim)).astype(jnp.bfloat16)
            k = matmul(normed, w_k_loc).astype(jnp.bfloat16)
            v = matmul(normed, w_v_loc).astype(jnp.bfloat16)
            q = rope(q.reshape(shard_rows, heads_loc, head_dim), cos_tab, sin_tab).reshape(shard_rows, kv_loc, group_size, head_dim)
            k = rope(k.reshape(shard_rows, kv_loc, head_dim), cos_tab, sin_tab)
            k_all = lax.all_gather(k, "sp", tiled=True)
            v_all = lax.all_gather(v.reshape(shard_rows, kv_loc, head_dim), "sp", tiled=True)
            mixed = attend(q, k_all, v_all, seg_q, seg_all, q_offset, layer % 2 == 0)
            part_sum = matmul(mixed, w_o[layer].reshape(heads_loc * head_dim, model)).astype(jnp.bfloat16)
            attn_out = lax.psum_scatter(part_sum, "tp", scatter_dimension=0, tiled=True)
            hidden = (x.astype(jnp.float32) + attn_out.astype(jnp.float32)).astype(jnp.bfloat16)
            normed = lax.all_gather(rms_norm(hidden, g_mlp[layer]), "tp", tiled=True)
            activation = (jax.nn.silu(matmul(normed, w_gate[layer])) * matmul(normed, w_up[layer])).astype(jnp.bfloat16)
            part_sum = matmul(activation, w_down[layer]).astype(jnp.bfloat16)
            mlp_out = lax.psum_scatter(part_sum, "tp", scatter_dimension=0, tiled=True)
            x = (hidden.astype(jnp.float32) + mlp_out.astype(jnp.float32)).astype(jnp.bfloat16)
        return x

    return jax.shard_map(local_fn, mesh=mesh, in_specs=in_specs, out_specs=row_spec, check_vma=False)
```

profile of v0, /device:TPU:1, one launch (start us, length us, event | category | flops | bytes accessed | tf_op | source)
XLA Modules:
  0.0 1357.7 jit_solution(4493224312441160569)
XLA Ops:
  6.6 7.6 fusion.431
  24.0 7.6 fusion.430
  33.8 16.7 %fusion.428 = (bf16[1,2048,8,128]{3,2,1,0:T(8,128)(2,1)}, bf16[1,2048,8,128]{3,2,1,0:T(8,128)(2,1)}, bf16[1,2048,8,128]{3,2,1,0:T(8,128)(2,1)}, bf16[1,2048,8,12...) fusion(bf16[6,2048,8,128]{3,2,1,0:T(8,128)(2,1)} %param.28), kind=kLoop, calls=%fused_computation.500 | loop fusion | bytes 50331648 | tf_op jit(solution)/shard_map/slice | solution.py:92
  51.6 69.2 %all-reduce = s32[8192]{0:T(1024)S(1)} all-reduce(s32[8192]{0:T(1024)S(1)} %dynamic-update-slice), channel_id=1, replica_groups=mesh['dp'=1,'sp'=64,'tp'=2] {'sp','tp'}, use_global_device_ids=true, to_apply=%add | all-reduce | flops 8192 | bytes 65536
  121.7 18.1 %fusion.429 = (bf16[1,8,128,2048]{3,2,1,0:T(8,128)(2,1)}, bf16[1,8,128,2048]{3,2,1,0:T(8,128)(2,1)}, bf16[1,8,128,2048]{3,2,1,0:T(8,128)(2,1)}, bf16[1,8,128,204...) fusion(bf16[6,8,128,2048]{3,2,1,0:T(8,128)(2,1)} %param.31), kind=kLoop, calls=%fused_computation.501 | loop fusion | bytes 50331648 | tf_op jit(solution)/shard_map/slice | solution.py:100
  139.8 4.1 copy.25
  143.9 13.9 %all-gather.31.cloned.1.call-done = bf16[8192,128]{1,0:T(8,128)(2,1)} async-done(((bf16[128,128]{1,0:T(8,128)(2,1)}), bf16[8192,128]{1,0:T(8,128)(2,1)}) %all-gather.31.cloned.1.call-update) | async-done | bytes 2097168 | tf_op jit(solution)/shard_map/all_gather | solution.py:98
  157.9 18.6 %while.84 = (s32[]{:T(128)}, bf16[4,32,1,8,128]{4,3,1,0,2:T(8,128)(2,1)S(1)}, s32[4]{0:T(128)S(1)}, s32[]{:T(128)}, bf16[8192,1,128]{2,0,1:T(8,128)(2,1)}, /*ind...) while((s32[]{:T(128)}, ...), condition=%wide.region_4.5_spmd, body=%wide.region_1.4_spmd.sunk | while | flops 140810816 | bytes 4272621 | solution.py:59
  176.4 3.7 convolution_convert_fusion.8
  180.9 10.5 reduce-scatter.13.cloned.1.call-done
  195.7 9.1 fusion.151
  204.9 9.4 fusion.204
  214.3 10.1 fusion.225
  226.4 10.1 reduce-scatter.15.cloned.1.call-done
  248.3 60.3 %all-gather.21.cloned.1.call-done = bf16[8192,1,128]{0,2,1:T(8,128)(2,1)} async-done(((bf16[128,1,128]{0,2,1:T(8,128)(2,1)}), bf16[8192,1,128]{0,2,1:T(8,128)(2,1)}) %all-gather.21.cloned.1.call-update) | async-done | bytes 2097168 | tf_op jit(solution)/shard_map/all_gather | solution.py:97
  308.6 3.2 copy.32
  311.8 63.0 %all-gather.33.cloned.1.call-done = bf16[8192,128]{1,0:T(8,128)(2,1)} async-done(((bf16[128,128]{1,0:T(8,128)(2,1)}), bf16[8192,128]{1,0:T(8,128)(2,1)}) %all-gather.33.cloned.1.call-update) | async-done | bytes 2097168 | tf_op jit(solution)/shard_map/all_gather | solution.py:98
  374.8 28.7 %while.85 = (s32[]{:T(128)}, bf16[4,32,1,8,128]{4,3,1,2,0:T(8,128)(2,1)S(1)}, s32[4]{0:T(128)S(1)}, s32[]{:T(128)}, s32[8192]{0:T(1024)S(1)}, /*index=5*/s32[4,3...) while((s32[]{:T(128)}, ...), condition=%wide.region_12.13_spmd, body=%wide.region_9.12_spmd.sunk | while | flops 1091345920 | bytes 38539124 | solution.py:59
  403.6 3.7 convolution_convert_fusion.7
  407.3 11.2 reduce-scatter.17.cloned.1.call-done
  423.2 9.1 fusion.145
  432.3 9.4 fusion.201
  441.8 10.1 fusion.228
  453.1 10.9 reduce-scatter.19.cloned.1.call-done
  474.5 60.3 %all-gather.23.cloned.1.call-done = bf16[8192,1,128]{0,2,1:T(8,128)(2,1)} async-done(((bf16[128,1,128]{0,2,1:T(8,128)(2,1)}), bf16[8192,1,128]{0,2,1:T(8,128)(2,1)}) %all-gather.23.cloned.1.call-update) | async-done | bytes 2097168 | tf_op jit(solution)/shard_map/all_gather | solution.py:97
  534.8 4.1 copy.36
  538.8 62.1 %all-gather.35.cloned.1.call-done = bf16[8192,128]{1,0:T(8,128)(2,1)} async-done(((bf16[128,128]{1,0:T(8,128)(2,1)}), bf16[8192,128]{1,0:T(8,128)(2,1)}) %all-gather.35.cloned.1.call-update) | async-done | bytes 2097168 | tf_op jit(solution)/shard_map/all_gather | solution.py:98
  601.0 18.1 %while.86 = (s32[]{:T(128)}, bf16[4,32,1,8,128]{4,3,1,0,2:T(8,128)(2,1)S(1)}, s32[4]{0:T(128)S(1)}, s32[]{:T(128)}, bf16[8192,1,128]{2,0,1:T(8,128)(2,1)}, /*ind...) while((s32[]{:T(128)}, ...), condition=%wide.region_20.21_spmd, body=%wide.region_17.20_spmd.sunk | while | flops 140810816 | bytes 4272621 | solution.py:59
  619.1 3.8 convolution_convert_fusion.6
  622.9 11.1 reduce-scatter.21.cloned.1.call-done
  638.9 9.1 fusion.139
  648.0 9.4 fusion.198
  657.5 10.1 fusion.231
  669.6 10.1 reduce-scatter.23.cloned.1.call-done
  691.5 60.1 %all-gather.25.cloned.1.call-done = bf16[8192,1,128]{0,2,1:T(8,128)(2,1)} async-done(((bf16[128,1,128]{0,2,1:T(8,128)(2,1)}), bf16[8192,1,128]{0,2,1:T(8,128)(2,1)}) %all-gather.25.cloned.1.call-update) | async-done | bytes 2097168 | tf_op jit(solution)/shard_map/all_gather | solution.py:97
  751.6 3.2 copy.43
  754.8 63.0 %all-gather.37.cloned.1.call-done = bf16[8192,128]{1,0:T(8,128)(2,1)} async-done(((bf16[128,128]{1,0:T(8,128)(2,1)}), bf16[8192,128]{1,0:T(8,128)(2,1)}) %all-gather.37.cloned.1.call-update) | async-done | bytes 2097168 | tf_op jit(solution)/shard_map/all_gather | solution.py:98
  817.9 28.4 %while.87 = (s32[]{:T(128)}, bf16[4,32,1,8,128]{4,3,1,2,0:T(8,128)(2,1)S(1)}, s32[4]{0:T(128)S(1)}, s32[]{:T(128)}, s32[8192]{0:T(1024)S(1)}, /*index=5*/s32[4,3...) while((s32[]{:T(128)}, ...), condition=%wide.region_28.29_spmd, body=%wide.region_25.28_spmd.sunk | while | flops 1091345920 | bytes 38539124 | solution.py:59
  846.3 3.7 convolution_convert_fusion.5
  850.0 11.1 reduce-scatter.25.cloned.1.call-done
  865.6 9.1 fusion.133
  874.7 9.4 fusion.195
  884.1 10.1 fusion.234
  895.7 10.7 reduce-scatter.27.cloned.1.call-done
  916.8 60.3 %all-gather.27.cloned.1.call-done = bf16[8192,1,128]{0,2,1:T(8,128)(2,1)} async-done(((bf16[128,1,128]{0,2,1:T(8,128)(2,1)}), bf16[8192,1,128]{0,2,1:T(8,128)(2,1)}) %all-gather.27.cloned.1.call-update) | async-done | bytes 2097168 | tf_op jit(solution)/shard_map/all_gather | solution.py:97
  977.1 4.1 copy.47
  981.2 62.1 %all-gather.39.cloned.1.call-done = bf16[8192,128]{1,0:T(8,128)(2,1)} async-done(((bf16[128,128]{1,0:T(8,128)(2,1)}), bf16[8192,128]{1,0:T(8,128)(2,1)}) %all-gather.39.cloned.1.call-update) | async-done | bytes 2097168 | tf_op jit(solution)/shard_map/all_gather | solution.py:98
  1043.4 18.4 %while.88 = (s32[]{:T(128)}, bf16[4,32,1,8,128]{4,3,1,0,2:T(8,128)(2,1)S(1)}, s32[4]{0:T(128)S(1)}, s32[]{:T(128)}, bf16[8192,1,128]{2,0,1:T(8,128)(2,1)}, /*ind...) while((s32[]{:T(128)}, ...), condition=%wide.region_36.37_spmd, body=%wide.region_33.36_spmd.sunk | while | flops 140810816 | bytes 4272621 | solution.py:59
  1061.8 3.8 convolution_convert_fusion.4
  1065.6 11.1 reduce-scatter.29.cloned.1.call-done
  1081.2 9.1 fusion.127
  1090.3 9.4 fusion.192
  1099.8 10.1 fusion.237
  1112.3 9.7 reduce-scatter.31.cloned.1.call-done
  1133.6 60.3 %all-gather.29.cloned.1.call-done = bf16[8192,1,128]{0,2,1:T(8,128)(2,1)} async-done(((bf16[128,1,128]{0,2,1:T(8,128)(2,1)}), bf16[8192,1,128]{0,2,1:T(8,128)(2,1)}) %all-gather.29.cloned.1.call-update) | async-done | bytes 2097168 | tf_op jit(solution)/shard_map/all_gather | solution.py:97
  1193.9 3.2 copy.54
  1197.1 63.1 %all-gather.41.cloned.1.call-done = bf16[8192,128]{1,0:T(8,128)(2,1)} async-done(((bf16[128,128]{1,0:T(8,128)(2,1)}), bf16[8192,128]{1,0:T(8,128)(2,1)}) %all-gather.41.cloned.1.call-update) | async-done | bytes 2097168 | tf_op jit(solution)/shard_map/all_gather | solution.py:98
  1260.3 28.3 %while.89 = (s32[]{:T(128)}, bf16[4,32,1,8,128]{4,3,1,2,0:T(8,128)(2,1)S(1)}, s32[4]{0:T(128)S(1)}, s32[]{:T(128)}, s32[8192]{0:T(1024)S(1)}, /*index=5*/s32[4,3...) while((s32[]{:T(128)}, ...), condition=%wide.region_44.45_spmd, body=%wide.region_41.44_spmd.sunk | while | flops 1091345920 | bytes 38539124 | solution.py:59
  1288.6 3.7 convolution_convert_fusion.3
  1292.4 11.1 reduce-scatter.33.cloned.1.call-done
  1308.1 9.1 fusion.121
  1317.2 9.5 fusion.189
  1326.7 10.1 fusion.240
  1336.8 12.1 reduce-scatter.35.cloned.1.call-done
  (493 shorter events, 231.4 us)
Async XLA Ops:
  6.5 133.3 %all-gather.19.cloned.1.call-start = ((), (), s32[]{:S(2)}) async-start(), calls=%async_computation.12 | async-start | bytes 2129920 | tf_op jit(solution)/shard_map/all_gather | solution.py:97
  6.5 7.6 copy-start.16
  6.6 8.3 copy-start
  6.6 11.8 copy-start.31
  6.6 13.0 copy-start.29
  24.0 133.8 %all-gather.31.cloned.1.call-start = ((), (), s32[]{:S(2)}) async-start(), calls=%async_computation.30 | async-start | bytes 2129920 | tf_op jit(solution)/shard_map/all_gather | solution.py:98
  33.7 157.6 %reduce-scatter.13.cloned.1.call-start = ((), (), s32[]{:S(2)}) async-start(), calls=%async_computation.13 | async-start | bytes 786432 | tf_op jit(solution)/shard_map/reduce_scatter | solution.py:101
  121.2 126.6 %copy-start.9 = (f32[128,64]{1,0:T(8,128)}, f32[128,64]{1,0:T(8,128)S(1)}, u32[]{:S(2)}) copy-start(f32[128,64]{1,0:T(8,128)S(1)} %get-tuple-element.1384) | copy-start | bytes 98308
  176.4 3.8 copy-start.17
  180.2 56.3 %reduce-scatter.15.cloned.1.call-start = ((), (), s32[]{:S(2)}) async-start(), calls=%async_computation.14 | async-start | bytes 786432 | tf_op jit(solution)/shard_map/reduce_scatter | solution.py:106
  214.3 22.2 %copy-start.12 = (bf16[64,2048]{1,0:T(8,128)(2,1)S(1)}, bf16[64,2048]{1,0:T(8,128)(2,1)}, u32[]{:S(2)}) copy-start(bf16[64,2048]{1,0:T(8,128)(2,1)} %reduce-scatter.13.cloned.1.call-done) | copy-start | bytes 786436
  224.4 84.2 %all-gather.21.cloned.1.call-start = ((), (), s32[]{:S(2)}) async-start(), calls=%async_computation.15 | async-start | bytes 2129920 | tf_op jit(solution)/shard_map/all_gather | solution.py:97
  242.6 132.2 %all-gather.33.cloned.1.call-start = ((), (), s32[]{:S(2)}) async-start(), calls=%async_computation.31 | async-start | bytes 2129920 | tf_op jit(solution)/shard_map/all_gather | solution.py:98
  244.8 173.8 %reduce-scatter.17.cloned.1.call-start = ((), (), s32[]{:S(2)}) async-start(), calls=%async_computation.16 | async-start | bytes 786432 | tf_op jit(solution)/shard_map/reduce_scatter | solution.py:101
  379.0 1.6 copy-start.27
  386.2 1.6 copy-start.27
  393.3 1.6 copy-start.27
  400.5 1.6 copy-start.27
  407.3 56.7 %reduce-scatter.19.cloned.1.call-start = ((), (), s32[]{:S(2)}) async-start(), calls=%async_computation.17 | async-start | bytes 786432 | tf_op jit(solution)/shard_map/reduce_scatter | solution.py:106
  441.8 10.2 copy-start.7
  441.8 23.5 %copy-start.24 = (f32[1,2048]{1,0:T(1,128)S(1)}, f32[1,2048]{1,0:T(1,128)}, u32[]{:S(2)}) copy-start(f32[1,2048]{1,0:T(1,128)} %get-tuple-element.1373) | copy-start | bytes 24580
  451.9 17.0 %copy-start.8 = (bf16[1,2048,2,128]{3,2,1,0:T(2,128)(2,1)S(1)}, bf16[1,2048,2,128]{3,2,1,0:T(2,128)(2,1)}, u32[]{:S(2)}) copy-start(bf16[1,2048,2,128]{3,2,1,0:T(2,128)(2,1)} %get-tuple-element.1338) | copy-start | bytes 3145732
  451.9 82.8 %all-gather.23.cloned.1.call-start = ((), (), s32[]{:S(2)}) async-start(), calls=%async_computation.18 | async-start | bytes 2129920 | tf_op jit(solution)/shard_map/all_gather | solution.py:97
  468.8 132.2 %all-gather.35.cloned.1.call-start = ((), (), s32[]{:S(2)}) async-start(), calls=%async_computation.32 | async-start | bytes 2129920 | tf_op jit(solution)/shard_map/all_gather | solution.py:98
  470.0 4.0 copy-start.10
  471.0 163.1 %reduce-scatter.21.cloned.1.call-start = ((), (), s32[]{:S(2)}) async-start(), calls=%async_computation.19 | async-start | bytes 786432 | tf_op jit(solution)/shard_map/reduce_scatter | solution.py:101
  619.1 16.1 %copy-start.25 = (f32[1,2048]{1,0:T(1,128)S(1)}, f32[1,2048]{1,0:T(1,128)}, u32[]{:S(2)}) copy-start(f32[1,2048]{1,0:T(1,128)} %get-tuple-element.1379) | copy-start | bytes 24580
  622.9 56.8 %reduce-scatter.23.cloned.1.call-start = ((), (), s32[]{:S(2)}) async-start(), calls=%async_computation.20 | async-start | bytes 786432 | tf_op jit(solution)/shard_map/reduce_scatter | solution.py:106
  657.5 10.2 copy-start.5
  657.5 22.2 %copy-start.14 = (bf16[64,2048]{1,0:T(8,128)(2,1)S(1)}, bf16[64,2048]{1,0:T(8,128)(2,1)}, u32[]{:S(2)}) copy-start(bf16[64,2048]{1,0:T(8,128)(2,1)} %reduce-scatter.21.cloned.1.call-done) | copy-start | bytes 786436
  657.5 23.4 %copy-start.22 = (f32[1,2048]{1,0:T(1,128)S(1)}, f32[1,2048]{1,0:T(1,128)}, u32[]{:S(2)}) copy-start(f32[1,2048]{1,0:T(1,128)} %get-tuple-element.1372) | copy-start | bytes 24580
  667.6 18.1 %copy-start.6 = (bf16[1,2048,2,128]{3,2,1,0:T(2,128)(2,1)S(1)}, bf16[1,2048,2,128]{3,2,1,0:T(2,128)(2,1)}, u32[]{:S(2)}) copy-start(bf16[1,2048,2,128]{3,2,1,0:T(2,128)(2,1)} %get-tuple-element.1337) | copy-start | bytes 3145732
  667.6 84.0 %all-gather.25.cloned.1.call-start = ((), (), s32[]{:S(2)}) async-start(), calls=%async_computation.21 | async-start | bytes 2129920 | tf_op jit(solution)/shard_map/all_gather | solution.py:97
  685.7 132.1 %all-gather.37.cloned.1.call-start = ((), (), s32[]{:S(2)}) async-start(), calls=%async_computation.33 | async-start | bytes 2129920 | tf_op jit(solution)/shard_map/all_gather | solution.py:98
  687.8 173.3 %reduce-scatter.25.cloned.1.call-start = ((), (), s32[]{:S(2)}) async-start(), calls=%async_computation.22 | async-start | bytes 786432 | tf_op jit(solution)/shard_map/reduce_scatter | solution.py:101
  821.9 1.6 copy-start.28
  829.0 1.6 copy-start.28
  836.1 1.6 copy-start.28
  843.2 1.6 copy-start.28
  846.2 16.1 %copy-start.23 = (f32[1,2048]{1,0:T(1,128)S(1)}, f32[1,2048]{1,0:T(1,128)}, u32[]{:S(2)}) copy-start(f32[1,2048]{1,0:T(1,128)} %get-tuple-element.1378) | copy-start | bytes 24580
  850.0 56.4 %reduce-scatter.27.cloned.1.call-start = ((), (), s32[]{:S(2)}) async-start(), calls=%async_computation.23 | async-start | bytes 786432 | tf_op jit(solution)/shard_map/reduce_scatter | solution.py:106
  884.1 10.4 copy-start.3
  884.1 23.5 %copy-start.20 = (f32[1,2048]{1,0:T(1,128)S(1)}, f32[1,2048]{1,0:T(1,128)}, u32[]{:S(2)}) copy-start(f32[1,2048]{1,0:T(1,128)} %get-tuple-element.1376) | copy-start | bytes 24580
  894.2 17.0 %copy-start.4 = (bf16[1,2048,2,128]{3,2,1,0:T(2,128)(2,1)S(1)}, bf16[1,2048,2,128]{3,2,1,0:T(2,128)(2,1)}, u32[]{:S(2)}) copy-start(bf16[1,2048,2,128]{3,2,1,0:T(2,128)(2,1)} %get-tuple-element.1336) | copy-start | bytes 3145732
  894.3 82.8 %all-gather.27.cloned.1.call-start = ((), (), s32[]{:S(2)}) async-start(), calls=%async_computation.24 | async-start | bytes 2129920 | tf_op jit(solution)/shard_map/all_gather | solution.py:97
  911.1 132.2 %all-gather.39.cloned.1.call-start = ((), (), s32[]{:S(2)}) async-start(), calls=%async_computation.34 | async-start | bytes 2129920 | tf_op jit(solution)/shard_map/all_gather | solution.py:98
  912.4 4.0 copy-start.11
  913.3 163.5 %reduce-scatter.29.cloned.1.call-start = ((), (), s32[]{:S(2)}) async-start(), calls=%async_computation.25 | async-start | bytes 786432 | tf_op jit(solution)/shard_map/reduce_scatter | solution.py:101
  1061.8 16.1 %copy-start.21 = (f32[1,2048]{1,0:T(1,128)S(1)}, f32[1,2048]{1,0:T(1,128)}, u32[]{:S(2)}) copy-start(f32[1,2048]{1,0:T(1,128)} %get-tuple-element.1382) | copy-start | bytes 24580
  1065.6 56.4 %reduce-scatter.31.cloned.1.call-start = ((), (), s32[]{:S(2)}) async-start(), calls=%async_computation.26 | async-start | bytes 786432 | tf_op jit(solution)/shard_map/reduce_scatter | solution.py:106
  1099.7 10.6 copy-start.1
  1099.8 22.2 %copy-start.13 = (bf16[64,2048]{1,0:T(8,128)(2,1)S(1)}, bf16[64,2048]{1,0:T(8,128)(2,1)}, u32[]{:S(2)}) copy-start(bf16[64,2048]{1,0:T(8,128)(2,1)} %reduce-scatter.29.cloned.1.call-done) | copy-start | bytes 786436
  1099.8 23.4 %copy-start.18 = (f32[1,2048]{1,0:T(1,128)S(1)}, f32[1,2048]{1,0:T(1,128)}, u32[]{:S(2)}) copy-start(f32[1,2048]{1,0:T(1,128)} %get-tuple-element.1371) | copy-start | bytes 24580
  1109.9 18.1 %copy-start.2 = (bf16[1,2048,2,128]{3,2,1,0:T(2,128)(2,1)S(1)}, bf16[1,2048,2,128]{3,2,1,0:T(2,128)(2,1)}, u32[]{:S(2)}) copy-start(bf16[1,2048,2,128]{3,2,1,0:T(2,128)(2,1)} %get-tuple-element.1335) | copy-start | bytes 3145732
  1109.9 84.0 %all-gather.29.cloned.1.call-start = ((), (), s32[]{:S(2)}) async-start(), calls=%async_computation.27 | async-start | bytes 2129920 | tf_op jit(solution)/shard_map/all_gather | solution.py:97
  1128.0 132.3 %all-gather.41.cloned.1.call-start = ((), (), s32[]{:S(2)}) async-start(), calls=%async_computation.35 | async-start | bytes 2129920 | tf_op jit(solution)/shard_map/all_gather | solution.py:98
  1130.1 173.4 %reduce-scatter.33.cloned.1.call-start = ((), (), s32[]{:S(2)}) async-start(), calls=%async_computation.28 | async-start | bytes 786432 | tf_op jit(solution)/shard_map/reduce_scatter | solution.py:101
  1264.4 1.6 copy-start.26
  1271.4 1.6 copy-start.26
  1278.5 1.6 copy-start.26
  1285.5 1.6 copy-start.26
  1288.6 16.1 %copy-start.19 = (f32[1,2048]{1,0:T(1,128)S(1)}, f32[1,2048]{1,0:T(1,128)}, u32[]{:S(2)}) copy-start(f32[1,2048]{1,0:T(1,128)} %get-tuple-element.1381) | copy-start | bytes 24580
  1292.3 56.5 %reduce-scatter.35.cloned.1.call-start = ((), (), s32[]{:S(2)}) async-start(), calls=%async_computation.29 | async-start | bytes 786432 | tf_op jit(solution)/shard_map/reduce_scatter | solution.py:106
  1326.7 22.2 %copy-start.15 = (bf16[64,2048]{1,0:T(8,128)(2,1)S(1)}, bf16[64,2048]{1,0:T(8,128)(2,1)}, u32[]{:S(2)}) copy-start(bf16[64,2048]{1,0:T(8,128)(2,1)} %reduce-scatter.33.cloned.1.call-done) | copy-start | bytes 786436
  (1 other events, 0.9 us)
Sparse Core Ops, SparseCore 0:
  24.1 67.2 all-gather.18
  94.3 63.4 all-gather.30
  180.3 10.9 reduce-scatter.12
  224.5 11.9 reduce-scatter.14
  242.7 65.7 all-gather.20
  311.3 63.4 all-gather.32
  407.4 11.1 reduce-scatter.16
  452.0 11.9 reduce-scatter.18
  468.9 65.7 all-gather.22
  537.5 63.4 all-gather.34
  623.0 11.0 reduce-scatter.20
  667.8 11.9 reduce-scatter.22
  685.8 65.7 all-gather.24
  754.3 63.4 all-gather.36
  850.1 10.9 reduce-scatter.24
  894.4 11.9 reduce-scatter.26
  911.3 65.7 all-gather.26
  979.8 63.4 all-gather.38
  1065.7 11.0 reduce-scatter.28
  1110.0 11.9 reduce-scatter.30
  1128.1 65.7 all-gather.28
  1196.7 63.4 all-gather.40
  1292.5 11.0 reduce-scatter.32
  1336.9 11.9 reduce-scatter.34
where the time goes:
time: 1370 us; the launch traced here: 1360 us
  waiting for transfers between devices  759 us (55%)
  matrix products  300 us (22%)
  local copies, waits for them, and re-layouts  109 us (8%)
  blocking collectives  99.2 us (7%)
  other arithmetic  55.8 us (4%)
  loops' own time  17 us (1%)
  between operations  15.7 us (1%)
    all_gather x6, waiting for transfers between devices, local_fn(): lax.all_gather(v.reshape(shard_rows, kv_loc, head_dim), 'sp', tiled=True)  327 us
    all_gather x6, waiting for transfers between devices, local_fn(): k_all = lax.all_gather(k, 'sp', tiled=True)  301 us
    dot_general x42, matrix products, matmul(): return jnp.dot(rows_in, weight, preferred_element_type=jnp.float32)  221 us
    unnamed x2, blocking collectives  71 us
    reduce_scatter x6, waiting for transfers between devices, local_fn(): attn_out = lax.psum_scatter(part_sum, 'tp', scatter_dimension=0, tiled=True)  66.2 us
    reduce_scatter x6, waiting for transfers between devices, local_fn(): mlp_out = lax.psum_scatter(part_sum, 'tp', scatter_dimension=0, tiled=True)  63.5 us
    dot_general x24, matrix products, one_block(): jnp.einsum('qgrd,kgd->qgrk', q_blk, k_blk, preferred_element_type=jnp.flo...  46.1 us
    dot_general x24, matrix products, one_block(): jnp.einsum('qgrk,kgd->qgrd', attn_probs, v_blk, preferred_element_type=jn...  33.3 us
  transfers between devices with their start and end apart: 24, of which 23 were waited for; matrix products, arithmetic and copies ran while one was open for 8% of the time, Pallas kernels for 0%

commit v1 on v0

v1 whole, which is shorter than its diff:
```python
import functools
import math

import jax
import jax.numpy as jnp
from jax import lax
from jax.experimental import pallas as pl
from jax.experimental.pallas import tpu as pltpu
from jax.sharding import PartitionSpec as P

EPS = 1e-6
ROPE_BASE = 10000.0
WINDOW = 1024
NEG = -1e30
MESH = pl.DeviceIdType.MESH
F32 = jnp.float32
BF16 = jnp.bfloat16
K_CUTS = (48, 48, 32)
V_CUTS = (32, 48, 48)
STRIDES = (1, 4, 16)
ORDERS = ((0, 1, 2), (1, 2, 0), (2, 0, 1))


def dot(a, b):
    return jnp.dot(a, b, preferred_element_type=F32)


def rms_norm(x, gain):
    x_wide = x.astype(F32)
    inv_rms = lax.rsqrt(jnp.mean(x_wide * x_wide, axis=-1, keepdims=True) + EPS)
    return (x_wide * inv_rms * gain.astype(F32)).astype(BF16)


def rope_tables(positions, head_dim):
    half_width = head_dim // 2
    inv_freq = ROPE_BASE ** (-jnp.arange(half_width, dtype=F32) / half_width)
    angles = positions.astype(F32)[:, None] * inv_freq[None, :]
    return jnp.cos(angles)[:, None, :], jnp.sin(angles)[:, None, :]


def rope(t, cos_tab, sin_tab):
    half_width = t.shape[-1] // 2
    t_wide = t.astype(F32)
    lower_half = t_wide[..., :half_width]
    upper_half = t_wide[..., half_width:]
    return jnp.concatenate([lower_half * cos_tab - upper_half * sin_tab, upper_half * cos_tab + lower_half * sin_tab], axis=-1).astype(BF16)


def build_queries(q_ref, cuts_ref, q_ext, q_base, heads, rows, hd):
    for h in range(heads):
        q_ext[0:hd, h * rows:(h + 1) * rows] = q_ref[:, h * hd:(h + 1) * hd].astype(F32).T.astype(BF16)
    cut0 = cuts_ref[0:1, :]
    cut1 = cuts_ref[1:2, :]
    q_pos = q_base + lax.broadcasted_iota(jnp.int32, (hd, rows), 1)
    seg_q = (q_pos >= cut0).astype(jnp.int32) + (q_pos >= cut1).astype(jnp.int32)
    feat = lax.broadcasted_iota(jnp.int32, (hd, rows), 0)
    val = jnp.where((feat < 4) & (feat != seg_q), NEG, 0.0).astype(BF16)
    for h in range(heads):
        q_ext[hd:2 * hd, h * rows:(h + 1) * rows] = val


def key_features(cuts_ref, k_base, keys, hd):
    cut0 = cuts_ref[0:1, :]
    cut1 = cuts_ref[1:2, :]
    k_pos = k_base + lax.broadcasted_iota(jnp.int32, (keys, hd), 0)
    seg_k = (k_pos >= cut0).astype(jnp.int32) + (k_pos >= cut1).astype(jnp.int32)
    seg_k = jnp.where(k_pos < 0, 3, seg_k)
    feat = lax.broadcasted_iota(jnp.int32, (keys, hd), 1)
    return jnp.where(feat == seg_k, 1.0, 0.0).astype(BF16)


def attend_tile(k, v_t, cuts_ref, q_ext, acc, m_ref, l_ref, k_base, q_base, rows, causal, windowed):
    keys, hd = k.shape
    cols = q_ext.shape[1]
    feats = key_features(cuts_ref, k_base, keys, hd)
    k_ext = jnp.concatenate([k, feats], axis=1)
    scale = math.log2(math.e) * hd ** -0.5
    s = dot(k_ext, q_ext[...])
    if causal or windowed:
        k_pos = k_base + lax.broadcasted_iota(jnp.int32, (keys, rows), 0)
        q_pos = q_base + lax.broadcasted_iota(jnp.int32, (keys, rows), 1)
        ok = (k_pos <= q_pos) if causal else (q_pos - k_pos < WINDOW)
        bias = jnp.where(ok, 0.0, NEG)
        s = jnp.concatenate([s[:, h * rows:(h + 1) * rows] + bias for h in range(cols // rows)], axis=1)
    m_prev = m_ref[...]
    m_new = jnp.maximum(m_prev, jnp.max(s, axis=0, keepdims=True))
    p = jnp.exp2((s - m_new) * scale)
    alpha = jnp.exp2((m_prev - m_new) * scale)
    m_ref[...] = m_new
    l_ref[...] = l_ref[...] * alpha + jnp.sum(p, axis=0, keepdims=True)
    acc[...] = acc[...] * alpha + dot(v_t, p.astype(BF16))


def start_state(acc, m_ref, l_ref):
    acc[...] = jnp.zeros_like(acc)
    m_ref[...] = jnp.full_like(m_ref, -3e37)
    l_ref[...] = jnp.zeros_like(l_ref)


def finish_state(mixed_ref, acc, l_ref, heads, rows, hd):
    inv = 1.0 / l_ref[...]
    for h in range(heads):
        cols = slice(h * rows, (h + 1) * rows)
        mixed_ref[:, h * hd:(h + 1) * hd] = (acc[:, cols] * inv[:, cols]).T.astype(BF16)


def window_kernel(sp_size, back, q_ref, kv_ref, cuts_ref, mixed_ref, buf, q_ext, acc, m_ref, l_ref, send_sem, recv_sem):
    rows, width = q_ref.shape
    hd = kv_ref.shape[1]
    heads = width // hd
    me = lax.axis_index("sp")
    barrier = pltpu.get_barrier_semaphore()
    for d in range(1, back + 1):
        pl.semaphore_signal(barrier, inc=1, device_id={"sp": lax.rem(me - d + sp_size, sp_size)}, device_id_type=MESH)
    pl.semaphore_wait(barrier, back)
    copies = []
    for d in range(1, back + 1):
        cp = pltpu.make_async_remote_copy(kv_ref, buf.at[back - d], send_sem.at[d - 1], recv_sem.at[back - d], device_id={"sp": lax.rem(me + d, sp_size)}, device_id_type=MESH)
        cp.start()
        copies.append(cp)
    q_base = me * rows
    build_queries(q_ref, cuts_ref, q_ext, q_base, heads, rows, hd)
    start_state(acc, m_ref, l_ref)
    attend_tile(kv_ref[0:rows, :], kv_ref[rows:2 * rows, :], cuts_ref, q_ext, acc, m_ref, l_ref, q_base, q_base, rows, True, False)
    per = 4
    for t in reversed(range(back // per)):
        for j in range(per):
            slot = t * per + j
            copies[back - slot - 1].wait_recv()
        k = jnp.concatenate([buf[t * per + j, 0:rows, :] for j in range(per)], axis=0)
        v_t = jnp.concatenate([buf[t * per + j, rows:2 * rows, :] for j in range(per)], axis=1)
        attend_tile(k, v_t, cuts_ref, q_ext, acc, m_ref, l_ref, q_base + (t * per - back) * rows, q_base, rows, False, t == 0)
    finish_state(mixed_ref, acc, l_ref, heads, rows, hd)
    for cp in copies:
        cp.wait_send()


def global_kernel(q_ref, kv_ref, cuts_ref, mixed_ref, buf_a, buf_b, buf_c, q_ext, acc, m_ref, l_ref, send_sem, recv_sem, own_sem):
    rows, width = q_ref.shape
    hd = kv_ref.shape[1]
    heads = width // hd
    me = lax.axis_index("sp")
    coords = (lax.rem(me, 4), lax.rem(me // 4, 4), me // 16)
    bufs = (buf_a, buf_b, buf_c)

    def peer(axis, step):
        c = coords[axis]
        return {"sp": me + (lax.rem(c + step + 4, 4) - c) * STRIDES[axis]}

    barrier = pltpu.get_barrier_semaphore()
    for axis in range(3):
        for step in (1, -1):
            pl.semaphore_signal(barrier, inc=1, device_id=peer(axis, step), device_id_type=MESH)
    offset = 0
    for o, (k_rows, v_rows) in enumerate(zip(K_CUTS, V_CUTS)):
        a1, a2, a3 = ORDERS[o]
        bufs[o][coords[a3], coords[a2], coords[a1]] = kv_ref[offset:offset + k_rows + v_rows, :]
        offset += k_rows + v_rows
    pl.semaphore_wait(barrier, 6)

    def part(o, phase, c, half):
        a1, a2, a3 = ORDERS[o]
        if phase == 0:
            cut = 48
            r = pl.ds(0, cut) if half == 0 else pl.ds(cut, K_CUTS[o] + V_CUTS[o] - cut)
            return bufs[o].at[coords[a3], coords[a2], c, r]
        if phase == 1:
            return bufs[o].at[coords[a3], c, pl.ds(2 * half, 2)]
        return bufs[o].at[c, pl.ds(2 * half, 2)]

    starts = (0, K_CUTS[0] + V_CUTS[0], 2 * hd - K_CUTS[2] - V_CUTS[2])

    def copy(o, phase, c, half, step, idx):
        ref = part(o, phase, c, half)
        src = ref
        if phase == 0 and idx < 4:
            src = kv_ref.at[pl.ds(starts[o] + 48 * half, 48 if half == 0 else K_CUTS[o] + V_CUTS[o] - 48)]
        return pltpu.make_async_remote_copy(src, ref, send_sem.at[o, phase, idx], recv_sem.at[o, phase, idx], device_id=peer(ORDERS[o][phase], step), device_id_type=MESH)

    def recv(o, phase, c, half, step, idx):
        ref = part(o, phase, c, half)
        return pltpu.make_async_remote_copy(ref, ref, send_sem.at[o, phase, idx], recv_sem.at[o, phase, idx], device_id=peer(ORDERS[o][phase], step), device_id_type=MESH)

    sent = []

    def go(*args):
        cp = copy(*args)
        cp.start()
        sent.append(cp)

    for phase in range(3):
        for o in range(3):
            c = coords[ORDERS[o][phase]]
            go(o, phase, c, 0, 1, 0)
            go(o, phase, c, 1, -1, 1)
            go(o, phase, c, 1, 1, 2)
            go(o, phase, c, 0, -1, 3)
        for o in range(3):
            c = coords[ORDERS[o][phase]]
            left, right = lax.rem(c + 3, 4), lax.rem(c + 1, 4)
            recv(o, phase, left, 0, 1, 0).wait_recv()
            go(o, phase, left, 0, 1, 4)
            recv(o, phase, right, 1, -1, 1).wait_recv()
            go(o, phase, right, 1, -1, 5)
        if phase == 0:
            build_queries(q_ref, cuts_ref, q_ext, me * rows, heads, rows, hd)
            start_state(acc, m_ref, l_ref)
        for o in range(3):
            c = coords[ORDERS[o][phase]]
            left, right, far = lax.rem(c + 3, 4), lax.rem(c + 1, 4), lax.rem(c + 2, 4)
            recv(o, phase, left, 1, 1, 2).wait_recv()
            recv(o, phase, right, 0, -1, 3).wait_recv()
            recv(o, phase, far, 0, 1, 4).wait_recv()
            recv(o, phase, far, 1, -1, 5).wait_recv()

    q_base = me * rows

    def tile(t, causal):
        y, z = lax.rem(t, 4), t // 4
        ks, vs = [], []
        for x in range(4):
            pieces = (buf_a.at[z, y, x], buf_b.at[x, z, y], buf_c.at[y, x, z])
            for o in range(3):
                ks.append(pieces[o][0:K_CUTS[o], :])
            vs.append(jnp.concatenate([pieces[o][K_CUTS[o]:K_CUTS[o] + V_CUTS[o], :] for o in range(3)], axis=0))
        attend_tile(jnp.concatenate(ks, axis=0), jnp.concatenate(vs, axis=1), cuts_ref, q_ext, acc, m_ref, l_ref, t * 4 * rows, q_base, rows, causal, False)

    @pl.loop(0, me // 4)
    def _(t):
        tile(t, False)

    tile(me // 4, True)
    finish_state(mixed_ref, acc, l_ref, heads, rows, hd)
    for cp in sent:
        cp.wait_send()


GU = 512
NS = 4
OC = 512
DC = 256


def mlp_kernel(layer, next_layer, mixed_ref, x_ref, gm_ref, ga_ref, wo, wg, wu, wd, xout, nout, wo_b, wg_b, wu_b, wd_b, act, o_snd, o_rcv, d_snd, d_rcv, hid, nrm, wo_sem, wg_sem, wu_sem, wd_sem, send_sem, recv_sem):
    rows, model = x_ref.shape
    ff = wg.shape[2]
    full = ff // GU
    rest = ff - full * GU
    n_o = model // OC
    n_d = model // DC
    other = 1 - lax.axis_index("tp")

    def wo_copy(c):
        return pltpu.make_async_copy(wo.at[layer, :, pl.ds(c * OC, OC)], wo_b.at[c], wo_sem.at[c])

    def gu_copies(i, slot):
        off = pl.multiple_of(i * GU, GU)
        return (
            pltpu.make_async_copy(wg.at[layer, :, pl.ds(off, GU)], wg_b.at[slot], wg_sem.at[slot]),
            pltpu.make_async_copy(wu.at[layer, :, pl.ds(off, GU)], wu_b.at[slot], wu_sem.at[slot]),
        )

    rest_slot = full % NS

    def rest_copies():
        return (
            pltpu.make_async_copy(wg.at[layer, :, pl.ds(full * GU, rest)], wg_b.at[rest_slot, :, pl.ds(0, rest)], wg_sem.at[rest_slot]),
            pltpu.make_async_copy(wu.at[layer, :, pl.ds(full * GU, rest)], wu_b.at[rest_slot, :, pl.ds(0, rest)], wu_sem.at[rest_slot]),
        )

    def wd_copy(n):
        return pltpu.make_async_copy(wd.at[layer, :, pl.ds(pl.multiple_of(n * DC, DC), DC)], wd_b.at[n], wd_sem.at[n])

    for c in range(n_o):
        wo_copy(c).start()
    for i in range(NS):
        for cp in gu_copies(i, i):
            cp.start()

    barrier = pltpu.get_barrier_semaphore()
    pl.semaphore_signal(barrier, inc=1, device_id={"tp": other}, device_id_type=MESH)
    pl.semaphore_wait(barrier, 1)

    def o_send(c):
        return pltpu.make_async_remote_copy(o_snd.at[c], o_rcv.at[c], send_sem.at[c], recv_sem.at[c], device_id={"tp": other}, device_id_type=MESH)

    def d_send(n):
        return pltpu.make_async_remote_copy(d_snd.at[n], d_rcv.at[n], send_sem.at[n_o + n], recv_sem.at[n_o + n], device_id={"tp": other}, device_id_type=MESH)

    for c in range(n_o):
        wo_copy(c).wait()
        o_snd[c] = dot(mixed_ref[...], wo_b[c]).astype(BF16)
        o_send(c).start()
    sq = jnp.zeros((rows, 1), F32)
    for c in range(n_o):
        o_send(c).wait_recv()
        cols = slice(c * OC, (c + 1) * OC)
        out = (o_snd[c].astype(F32) + o_rcv[c].astype(F32)).astype(BF16)
        h = (x_ref[:, cols].astype(F32) + out.astype(F32)).astype(BF16)
        hid[:, cols] = h
        h = h.astype(F32)
        sq += jnp.sum(h * h, axis=1, keepdims=True)
    inv = lax.rsqrt(sq / model + EPS)
    for c in range(n_o):
        cols = slice(c * OC, (c + 1) * OC)
        nrm[:, cols] = (hid[:, cols].astype(F32) * inv * gm_ref[layer:layer + 1, cols].astype(F32)).astype(BF16)

    def gate_up(g_w, u_w):
        g = dot(nrm[...], g_w)
        u = dot(nrm[...], u_w)
        return (jax.nn.silu(g) * u).astype(BF16)

    @pl.loop(0, full)
    def _(i):
        slot = lax.rem(i, NS)
        for cp in gu_copies(i, slot):
            cp.wait()
        act[:, pl.ds(pl.multiple_of(i * GU, GU), GU)] = gate_up(wg_b[slot], wu_b[slot])

        @pl.when(i < full - NS)
        def _():
            for cp in gu_copies(i + NS, slot):
                cp.start()

        if rest:
            @pl.when(i == full - NS)
            def _():
                for cp in rest_copies():
                    cp.start()

        @pl.when(i < n_d)
        def _():
            wd_copy(i).start()

    if rest:
        for cp in rest_copies():
            cp.wait()
        act[:, full * GU:ff] = gate_up(wg_b[rest_slot, :, 0:rest], wu_b[rest_slot, :, 0:rest])

    @pl.loop(0, n_d)
    def _(n):
        wd_copy(n).wait()
        d_snd[n] = dot(act[...], wd_b[n]).astype(BF16)
        d_send(n).start()

    sq = jnp.zeros((rows, 1), F32)
    for n in range(n_d):
        d_send(n).wait_recv()
        cols = slice(n * DC, (n + 1) * DC)
        out = (d_snd[n].astype(F32) + d_rcv[n].astype(F32)).astype(BF16)
        h = (hid[:, cols].astype(F32) + out.astype(F32)).astype(BF16)
        xout[:, cols] = h
        h = h.astype(F32)
        sq += jnp.sum(h * h, axis=1, keepdims=True)
    inv = lax.rsqrt(sq / model + EPS)
    for n in range(n_d):
        cols = slice(n * DC, (n + 1) * DC)
        nout[:, cols] = (xout[:, cols].astype(F32) * inv * ga_ref[next_layer:next_layer + 1, cols].astype(F32)).astype(BF16)
    for c in range(n_o):
        o_send(c).wait_send()
    for n in range(n_d):
        d_send(n).wait_send()


VM = pl.BlockSpec(memory_space=pltpu.VMEM)
ANY = pl.BlockSpec(memory_space=pl.ANY)


def call_mlp(layer, next_layer, cid, mixed, x, g_mlp, g_attn, w_o, w_gate, w_up, w_down):
    rows, model = x.shape
    ff = w_gate.shape[2]
    depth = w_o.shape[1]
    n_o, n_d = model // OC, model // DC
    return pl.pallas_call(
        functools.partial(mlp_kernel, layer, next_layer),
        out_shape=[jax.ShapeDtypeStruct((rows, model), BF16)] * 2,
        in_specs=[VM] * 4 + [ANY] * 4,
        out_specs=[VM] * 2,
        scratch_shapes=[
            pltpu.VMEM((n_o, depth, OC), BF16),
            pltpu.VMEM((NS, model, GU), BF16),
            pltpu.VMEM((NS, model, GU), BF16),
            pltpu.VMEM((n_d, ff, DC), BF16),
            pltpu.VMEM((rows, ff), BF16),
            pltpu.VMEM((n_o, rows, OC), BF16),
            pltpu.VMEM((n_o, rows, OC), BF16),
            pltpu.VMEM((n_d, rows, DC), BF16),
            pltpu.VMEM((n_d, rows, DC), BF16),
            pltpu.VMEM((rows, model), BF16),
            pltpu.VMEM((rows, model), BF16),
            pltpu.SemaphoreType.DMA((n_o,)),
            pltpu.SemaphoreType.DMA((NS,)),
            pltpu.SemaphoreType.DMA((NS,)),
            pltpu.SemaphoreType.DMA((n_d,)),
            pltpu.SemaphoreType.DMA((n_o + n_d,)),
            pltpu.SemaphoreType.DMA((n_o + n_d,)),
        ],
        compiler_params=pltpu.CompilerParams(collective_id=cid, has_side_effects=True, vmem_limit_bytes=58 * 2**20),
        cost_estimate=pl.CostEstimate(flops=2 * rows * model * (3 * ff + depth), bytes_accessed=2 * model * (3 * ff + depth), transcendentals=0),
        name=f"mlp_{layer}",
    )(mixed, x, g_mlp, g_attn, w_o, w_gate, w_up, w_down)


def call_attention(windowed, cid, sp_size, q, kv, cuts):
    rows, width = q.shape
    hd = kv.shape[1]
    cols = width // hd * rows
    tail = [
        pltpu.VMEM((2 * hd, cols), BF16),
        pltpu.VMEM((hd, cols), F32),
        pltpu.VMEM((1, cols), F32),
        pltpu.VMEM((1, cols), F32),
    ]
    if windowed:
        back = WINDOW // rows
        body = functools.partial(window_kernel, sp_size, back)
        scratch = [pltpu.VMEM((back, 2 * rows, hd), BF16)] + tail + [pltpu.SemaphoreType.DMA((back,)), pltpu.SemaphoreType.DMA((back,))]
    else:
        body = global_kernel
        scratch = [pltpu.VMEM((4, 4, 4, a + b, hd), BF16) for a, b in zip(K_CUTS, V_CUTS)] + tail
        scratch += [pltpu.SemaphoreType.DMA((3, 3, 6)), pltpu.SemaphoreType.DMA((3, 3, 6)), pltpu.SemaphoreType.DMA]
    return pl.pallas_call(
        body,
        out_shape=jax.ShapeDtypeStruct((rows, width), BF16),
        in_specs=[VM] * 3,
        out_specs=VM,
        scratch_shapes=scratch,
        compiler_params=pltpu.CompilerParams(collective_id=cid, has_side_effects=True, vmem_limit_bytes=40 * 2**20),
        name="attn_w" if windowed else "attn_g",
    )(q, kv, cuts)


def solution(mesh):
    sp_size = mesh.shape["sp"]
    row_spec = P(("dp", "sp", "tp"), None)
    id_spec = P(("dp", "sp", "tp"))
    whole = P()
    in_specs = (row_spec, id_spec, id_spec, whole, P(None, None, "tp", None), whole, whole, P(None, "tp", None, None), whole, P(None, None, "tp"), P(None, None, "tp"), P(None, "tp", None))

    def local_fn(x, segment_ids, positions, g_attn, w_q, w_k, w_v, w_o, g_mlp, w_gate, w_up, w_down):
        tp_idx = lax.axis_index("tp")
        layers, model, heads_loc, head_dim = w_q.shape
        own_rows = x.shape[0]
        counts = jnp.stack([jnp.sum((segment_ids < 1).astype(jnp.int32)), jnp.sum((segment_ids < 2).astype(jnp.int32))])
        counts = lax.psum(counts, ("dp", "sp", "tp"))
        cuts = jnp.broadcast_to(jnp.pad(counts, (0, 6))[:, None], (8, head_dim))
        pos_shard = lax.all_gather(positions, "tp", tiled=True)
        cos_tab, sin_tab = rope_tables(pos_shard, head_dim)
        w_kv = jnp.concatenate([lax.dynamic_index_in_dim(w_k, tp_idx, 2, False), lax.dynamic_index_in_dim(w_v, tp_idx, 2, False)], axis=2)
        w_o2 = w_o.reshape(layers, heads_loc * head_dim, model)
        x = lax.all_gather(x, "tp", tiled=True)
        rows = x.shape[0]
        normed = rms_norm(x, g_attn[0])
        for layer in range(layers):
            windowed = layer % 2 == 0
            q = dot(normed, w_q[layer].reshape(model, heads_loc * head_dim)).astype(BF16)
            kv = dot(normed, w_kv[layer]).astype(BF16)
            q = rope(q.reshape(rows, heads_loc, head_dim), cos_tab, sin_tab).reshape(rows, heads_loc * head_dim)
            k = rope(kv[:, None, :head_dim], cos_tab, sin_tab).reshape(rows, head_dim)
            v_t = kv[:, head_dim:].T
            if windowed:
                kv = jnp.concatenate([k, v_t], axis=0)
            else:
                pieces, ko, vo = [], 0, 0
                for a, b in zip(K_CUTS, V_CUTS):
                    pieces += [k[ko:ko + a], v_t[vo:vo + b]]
                    ko, vo = ko + a, vo + b
                kv = jnp.concatenate(pieces, axis=0)
            mixed = call_attention(windowed, 10 if windowed else 11, sp_size, q, kv, cuts)
            x, normed = call_mlp(layer, (layer + 1) % layers, layer, mixed, x, g_mlp, g_attn, w_o2, w_gate, w_up, w_down)
        return lax.dynamic_slice_in_dim(x, tp_idx * own_rows, own_rows, 0)

    return jax.shard_map(local_fn, mesh=mesh, in_specs=in_specs, out_specs=row_spec, check_vma=False)
```

time: 1370 us -> 558 us (0.41)
  the two profiles are of different devices: /device:TPU:1 before, /device:TPU:121 now
where the time goes in v1:
time: 558 us; the launch traced here: 552 us
  Pallas kernels  385 us (69%)
  blocking collectives  68.8 us (12%)
  local copies, waits for them, and re-layouts  55.3 us (10%)
  matrix products  24.3 us (4%)
  other arithmetic  16.9 us (3%)
    pallas_call x6, Pallas kernels, call_mlp(): pl.pallas_call(functools.partial(mlp_kernel, layer, next_layer), out_shap...  206 us
    pallas_call x6, Pallas kernels, call_attention(): pl.pallas_call(body, out_shape=jax.ShapeDtypeStruct((rows, width), BF16),...  179 us
    psum x1, blocking collectives, local_fn(): counts = lax.psum(counts, ('dp', 'sp', 'tp'))  64.4 us
    dot_general x12, matrix products, dot(): return jnp.dot(a, b, preferred_element_type=F32)  24.3 us
    slice x1, local copies, waits for them, and re-layouts, local_fn(): w_q[layer].reshape(model, heads_loc * head_dim)  16.8 us
    dynamic_slice x1, local copies, waits for them, and re-layouts, local_fn(): lax.dynamic_index_in_dim(w_v, tp_idx, 2, False)  14.5 us

profile of v1, /device:TPU:121, one launch (start us, length us, event | category | flops | bytes accessed | tf_op | source)
XLA Modules:
  0.0 552.0 jit_solution(17985865632316060724)
XLA Ops:
  0.0 14.5 %constant_dynamic-slice_fusion.1 = (bf16[6,2048,1,128]{3,2,1,0:T(2,128)(2,1)S(1)}, bf16[6,2048,1,128]{3,2,1,0:T(2,128)(2,1)S(1)}) fusion(bf16[6,2048,2,128]{3,2,1,0:T(2,128)(2,1)} %param.18, s32[]{:T(128)S(6)} %select_n.8, bf16[6,2048,2,128]{3,2,1,0:T(2,128)(2,1)} %param.17), kind=kLoop, calls=%fused_computation.198 | loop fusion | bytes 12582916 | tf_op jit(solution)/shard_map/jit(dynamic_index_in_dim)/dynamic_slice | solution.py:449
  15.9 2.6 all_gather.6.x_ref
  18.7 0.8 slice_convert_fusion
  21.4 1.9 all-reduce.1
  24.4 0.9 multiply_cosine_fusion
  25.4 16.8 %fusion.151 = (bf16[1,2048,8,128]{3,2,1,0:T(8,128)(2,1)}, bf16[1,2048,8,128]{3,2,1,0:T(8,128)(2,1)}, bf16[1,2048,8,128]{3,2,1,0:T(8,128)(2,1)}, bf16[1,2048,8,12...) fusion(bf16[6,2048,8,128]{3,2,1,0:T(8,128)(2,1)} %param.16), kind=kLoop, calls=%fused_computation.211 | loop fusion | bytes 50331648 | tf_op jit(solution)/shard_map/slice | solution.py:456
  42.3 0.8 fusion.24
  43.7 0.7 fusion.143
  44.3 1.4 pad_add_fusion
  45.7 64.4 %psum.7 = s32[2]{0:T(128)S(1)} all-reduce(s32[2]{0:T(128)S(1)} %pad_add_fusion), channel_id=1, replica_groups=mesh['dp'=1,'sp'=64,'tp'=2] {'dp','sp','tp'}, use_global_device_ids=true, to_apply=%region_3.4 | all-reduce | flops 2 | bytes 16 | tf_op jit(solution)/shard_map/psum | solution.py:445
  110.2 14.3 %attn_w.3.mixed_ref = bf16[128,1024]{1,0:T(8,128)(2,1)S(1)} custom-call(bf16[128,1024]{1,0:T(8,128)(2,1)S(1)} %bitcast.221, bf16[256,128]{1,0:T(8,128)(2,1)S(1)} %copy.101.kv_ref, s32[8,128]{1,0:T(8,128)S(1)} %broadcast_in_dim.2.cuts_ref), custom_call_target="tpu_custom_call" | custom-call | tf_op jit(solution)/shard_map/attn_w/pallas_call | solution.py:422
  124.5 0.7 copy-done.5
  125.2 32.1 %mlp_0.1 = (bf16[128,2048]{1,0:T(8,128)(2,1)}, bf16[128,2048]{1,0:T(8,128)(2,1)}) custom-call(bf16[128,1024]{1,0:T(8,128)(2,1)} %copy-done.5, bf16[128,2048]{1,0:T(8,128)(2,1)} %copy-done.7, bf16[6,2048]{1,0:T(8,128)(2,1)} %gm_ref.11, bf16[6,2048]{1,0:T(8,128)(2,1)} %ga_ref.11, bf16[6,1024,2048]{2,1,0:T(8,128)(2,1)} %bitcast.227, ...), custom_call_target="tpu_custom_call" | custom-call | flops 9193914368 | bytes 71827456 | tf_op jit(solution)/shard_map/mlp_0/pallas_call | solution.py:374
  157.3 1.5 convolution_convert_fusion.4
  158.9 0.7 slice_multiply_fusion.3
  159.6 0.9 copy.104
  160.6 0.9 copy.106
  161.7 0.8 copy.107
  162.6 0.7 fusion.137
  163.3 0.7 fusion.111
  164.0 0.7 fusion.153
  164.7 0.9 concatenate.122
  165.7 3.1 fusion.33
  169.4 46.6 %attn_g.3.mixed_ref = bf16[128,1024]{1,0:T(8,128)(2,1)S(1)} custom-call(bf16[128,1024]{1,0:T(8,128)(2,1)S(1)} %bitcast.223, bf16[256,128]{1,0:T(8,128)(2,1)S(1)} %copy.108.kv_ref, s32[8,128]{1,0:T(8,128)S(1)} %broadcast_in_dim.2.cuts_ref), custom_call_target="tpu_custom_call" | custom-call | tf_op jit(solution)/shard_map/attn_g/pallas_call | solution.py:422
  216.1 0.7 copy-done.1
  216.8 36.7 %mlp_1.1 = (bf16[128,2048]{1,0:T(8,128)(2,1)}, bf16[128,2048]{1,0:T(8,128)(2,1)}) custom-call(bf16[128,1024]{1,0:T(8,128)(2,1)} %copy-done.1, bf16[128,2048]{1,0:T(8,128)(2,1)} %get-tuple-element.17.x_ref, bf16[6,2048]{1,0:T(8,128)(2,1)} %gm_ref.11, bf16[6,2048]{1,0:T(8,128)(2,1)} %ga_ref.11, bf16[6,1024,2048]{2,1,0:T(8,128)(2,1)} %bitcast.228, ...), custom_call_target="tpu_custom_call" | custom-call | flops 9193914368 | bytes 71827456 | tf_op jit(solution)/shard_map/mlp_1/pallas_call | solution.py:374
  253.5 1.5 convolution_convert_fusion.3
  255.6 0.7 fusion.129
  256.3 0.9 copy.111
  257.3 0.8 fusion.141
  258.1 0.8 copy.114
  259.0 0.8 pad_maximum_fusion.8
  259.9 3.1 fusion.42
  263.6 14.7 %attn_w.4.mixed_ref = bf16[128,1024]{1,0:T(8,128)(2,1)S(1)} custom-call(bf16[128,1024]{1,0:T(8,128)(2,1)S(1)} %bitcast.224, bf16[256,128]{1,0:T(8,128)(2,1)S(1)} %copy.115.kv_ref, s32[8,128]{1,0:T(8,128)S(1)} %broadcast_in_dim.2.cuts_ref), custom_call_target="tpu_custom_call" | custom-call | tf_op jit(solution)/shard_map/attn_w/pallas_call | solution.py:422
  278.3 0.7 copy-done.2
  279.0 33.1 %mlp_2.1 = (bf16[128,2048]{1,0:T(8,128)(2,1)}, bf16[128,2048]{1,0:T(8,128)(2,1)}) custom-call(bf16[128,1024]{1,0:T(8,128)(2,1)} %copy-done.2, bf16[128,2048]{1,0:T(8,128)(2,1)} %get-tuple-element.19.x_ref, bf16[6,2048]{1,0:T(8,128)(2,1)} %gm_ref.11, bf16[6,2048]{1,0:T(8,128)(2,1)} %ga_ref.11, bf16[6,1024,2048]{2,1,0:T(8,128)(2,1)} %bitcast.229, ...), custom_call_target="tpu_custom_call" | custom-call | flops 9193914368 | bytes 71827456 | tf_op jit(solution)/shard_map/mlp_2/pallas_call | solution.py:374
  312.1 1.5 convolution_convert_fusion.2
  313.6 0.7 slice_multiply_fusion.1
  314.4 0.9 copy.118
  315.3 0.9 copy.120
  316.4 0.8 copy.121
  317.3 0.7 fusion.134
  318.0 0.7 fusion.152
  318.7 1.5 concatenate.130
  320.3 0.9 copy.122.kv_ref
  321.2 3.1 fusion.51
  324.9 43.7 %attn_g.4.mixed_ref = bf16[128,1024]{1,0:T(8,128)(2,1)S(1)} custom-call(bf16[128,1024]{1,0:T(8,128)(2,1)S(1)} %bitcast.225, bf16[256,128]{1,0:T(8,128)(2,1)S(1)} %copy.122.kv_ref, s32[8,128]{1,0:T(8,128)S(1)} %broadcast_in_dim.2.cuts_ref), custom_call_target="tpu_custom_call" | custom-call | tf_op jit(solution)/shard_map/attn_g/pallas_call | solution.py:422
  368.6 0.7 copy-done.3
  369.3 36.3 %mlp_3.1 = (bf16[128,2048]{1,0:T(8,128)(2,1)}, bf16[128,2048]{1,0:T(8,128)(2,1)}) custom-call(bf16[128,1024]{1,0:T(8,128)(2,1)} %copy-done.3, bf16[128,2048]{1,0:T(8,128)(2,1)} %get-tuple-element.21.x_ref, bf16[6,2048]{1,0:T(8,128)(2,1)} %gm_ref.11, bf16[6,2048]{1,0:T(8,128)(2,1)} %ga_ref.11, bf16[6,1024,2048]{2,1,0:T(8,128)(2,1)} %bitcast.230, ...), custom_call_target="tpu_custom_call" | custom-call | flops 9193914368 | bytes 71827456 | tf_op jit(solution)/shard_map/mlp_3/pallas_call | solution.py:374
  405.6 1.5 convolution_convert_fusion.1
  407.7 0.7 fusion.130
  408.4 0.9 copy.125
  409.6 0.8 copy.128
  410.5 0.8 pad_maximum_fusion.9
  411.4 3.1 fusion.60
  415.1 15.4 %attn_w.5.mixed_ref = bf16[128,1024]{1,0:T(8,128)(2,1)S(1)} custom-call(bf16[128,1024]{1,0:T(8,128)(2,1)S(1)} %bitcast.226, bf16[256,128]{1,0:T(8,128)(2,1)S(1)} %copy.129.kv_ref, s32[8,128]{1,0:T(8,128)S(1)} %broadcast_in_dim.2.cuts_ref), custom_call_target="tpu_custom_call" | custom-call | tf_op jit(solution)/shard_map/attn_w/pallas_call | solution.py:422
  430.5 0.7 copy-done.4
  431.2 31.8 %mlp_4.1 = (bf16[128,2048]{1,0:T(8,128)(2,1)}, bf16[128,2048]{1,0:T(8,128)(2,1)}) custom-call(bf16[128,1024]{1,0:T(8,128)(2,1)} %copy-done.4, bf16[128,2048]{1,0:T(8,128)(2,1)} %get-tuple-element.23.x_ref, bf16[6,2048]{1,0:T(8,128)(2,1)} %gm_ref.11, bf16[6,2048]{1,0:T(8,128)(2,1)} %ga_ref.11, bf16[6,1024,2048]{2,1,0:T(8,128)(2,1)} %bitcast.231, ...), custom_call_target="tpu_custom_call" | custom-call | flops 9193914368 | bytes 71827456 | tf_op jit(solution)/shard_map/mlp_4/pallas_call | solution.py:374
  463.0 1.7 convolution_convert_fusion
  465.5 3.1 fusion.69
  469.2 44.3 %attn_g.5.mixed_ref = bf16[128,1024]{1,0:T(8,128)(2,1)S(1)} custom-call(bf16[128,1024]{1,0:T(8,128)(2,1)S(1)} %bitcast.222, bf16[256,128]{1,0:T(8,128)(2,1)S(1)} %constant_dynamic-update-slice_fusion.kv_ref, s32[8,128]{1,0:T(8,128)S(1)} %broadcast_in_dim.2.cuts_ref), custom_call_target="tpu_custom_call" | custom-call | tf_op jit(solution)/shard_map/attn_g/pallas_call | solution.py:422
  513.5 0.7 copy-done
  514.2 35.9 %mlp_5.1 = (bf16[128,2048]{1,0:T(8,128)(2,1)}, bf16[128,2048]{1,0:T(8,128)(2,1)}) custom-call(bf16[128,1024]{1,0:T(8,128)(2,1)} %copy-done, bf16[128,2048]{1,0:T(8,128)(2,1)} %get-tuple-element.25.x_ref, bf16[6,2048]{1,0:T(8,128)(2,1)} %gm_ref.11, bf16[6,2048]{1,0:T(8,128)(2,1)} %ga_ref.11, bf16[6,1024,2048]{2,1,0:T(8,128)(2,1)} %bitcast.232, ...), custom_call_target="tpu_custom_call" | custom-call | flops 9193914368 | bytes 71827456 | tf_op jit(solution)/shard_map/mlp_5/pallas_call | solution.py:374
  550.2 1.7 constant_dynamic-slice_fusion
  (113 shorter events, 10.7 us)
Async XLA Ops:
  14.9 1.0 copy-start.15
  15.3 4.5 copy-start.6
  15.9 4.0 copy-start.22
  15.9 5.3 copy-start.20
  18.5 1.0 copy-start.7
  18.7 4.6 copy-start.18
  23.2 1.1 copy-start.16
  23.5 0.7 copy-start.11
  23.7 0.6 copy-start.13
  25.4 17.8 %copy-start.9 = (f32[128,64]{1,0:T(8,128)}, f32[128,64]{1,0:T(8,128)S(1)}, u32[]{:S(2)}) copy-start(f32[128,64]{1,0:T(8,128)S(1)} %get-tuple-element.89) | copy-start | bytes 98308
  25.4 16.9 %copy-start.8 = (bf16[128,2048]{1,0:T(8,128)(2,1)S(1)}, bf16[128,2048]{1,0:T(8,128)(2,1)}, u32[]{:S(2)}) copy-start(bf16[128,2048]{1,0:T(8,128)(2,1)} %copy-done.7) | copy-start | bytes 1572868
  25.4 16.9 %copy-start.19 = (f32[128]{0:T(128)S(1)}, f32[128]{0:T(128)}, u32[]{:S(2)}) copy-start(f32[128]{0:T(128)} %copy-done.18) | copy-start | bytes 1540
  42.3 1.4 copy-start.21
  124.5 0.7 copy-start.5
  157.3 1.6 copy-start.12
  157.3 1.6 copy-start.14
  157.3 4.2 copy-start.17
  159.6 9.3 %copy-start.10 = (f32[128,64]{1,0:T(8,128)S(1)}, f32[128,64]{1,0:T(8,128)}, u32[]{:S(2)}) copy-start(f32[128,64]{1,0:T(8,128)} %copy-done.9) | copy-start | bytes 98308
  216.1 0.7 copy-start.1
  278.3 0.7 copy-start.2
  368.6 0.7 copy-start.3
  430.5 0.7 copy-start.4
  513.5 0.7 copy-start
